TPU v7x, 32 devices: a whole 2x2x4 slice. The times are simulated.
32 devices in a mesh: groups: 2 (over y), tensor: 4 (over z), frames: 4 (over x, core).
Axes of the slice: x: 2, y: 2, z: 4, core: 2. Of those that a mesh axis runs over, the one named last changes fastest.
Arguments:
- patches: bfloat16 [256, 16, 3072], P('tensor', ('groups', 'frames')), parts along dimension 1, may hold values from -12 to 12
- ln_gain: float32 [3072], replicated, may hold values from 0.5 to 1.5
- in_weight: bfloat16 [3072, 4, 768], P('frames', 'tensor'), may hold values from -0.109375 to 0.109375
- q_gain: float32 [4, 128], P('tensor'), may hold values from 0.1 to 1.9
- k_gain: float32 [4, 128], P('tensor'), may hold values from 0.1 to 1.9
- out_weight: bfloat16 [4, 512, 3072], P('tensor', None, 'frames'), may hold values from -0.25 to 0.25
Outputs:
- encoded: bfloat16 [256, 16, 3072], P('tensor', ('groups', 'frames')), parts along dimension 1
There are 2 independent parts, one for each index of `groups`. A program takes and returns all parts, laid end to end along the dimension named above; an argument that names none is the same for every part. Nothing has to cross between parts.
All inputs are finite; a program needn't handle non-finite values.
Results may differ from a plain program's by a relative error of at most 0.022.
Values may be sent and summed in bfloat16 or wider, within the bound.
No kernel may reach another device: no remote copies, remote signals or barrier semaphores. Data moves between devices by JAX's collectives and lax.ppermute only.
A program may use at most 64 MiB of HBM per device.

v0:
```python
import math
import jax
import jax.numpy as jnp
from jax import lax
from jax.sharding import PartitionSpec as P


def layer_norm(values, gain_vec):
    mean_val = jnp.mean(values, axis=-1, keepdims=True)
    centered = values - mean_val
    variance = jnp.mean(centered * centered, axis=-1, keepdims=True)
    return centered * lax.rsqrt(variance + 1e-06) * gain_vec


def local(patches, ln_gain, in_weight, q_gain, k_gain, out_weight):
    head_dim = q_gain.shape[1]
    normed = layer_norm(patches.astype(jnp.float32), ln_gain).astype(jnp.bfloat16)
    in_local = in_weight[:, 0, :]
    out_local = out_weight[0]
    every_patch = lax.all_gather(normed, "tensor", axis=0, tiled=True)
    joined_cols = jnp.einsum(
        "qye,ea->qya",
        every_patch,
        lax.all_gather(in_local, "frames", axis=0, tiled=True),
        preferred_element_type=jnp.float32,
    )
    query_slice = layer_norm(joined_cols[..., :head_dim], q_gain[0])
    key_slice = layer_norm(joined_cols[..., head_dim : 2 * head_dim], k_gain[0])
    value_slice = joined_cols[..., 2 * head_dim : 3 * head_dim]
    hidden = jax.nn.gelu(joined_cols[..., 3 * head_dim :], approximate=False)
    prepared = jnp.concatenate([query_slice, key_slice, value_slice, hidden], axis=-1).astype(
        jnp.bfloat16
    )
    query_slice = prepared[..., :head_dim]
    key_slice = prepared[..., head_dim : 2 * head_dim]
    value_slice = prepared[..., 2 * head_dim : 3 * head_dim]
    attention_logits = jnp.einsum(
        "ldg,bdg->dlb", query_slice, key_slice, preferred_element_type=jnp.float32
    ) * (1.0 / math.sqrt(head_dim))
    exponent_scores = jnp.exp(attention_logits)
    softmax_total = jnp.sum(exponent_scores, axis=-1)
    attention_output = jnp.einsum(
        "jdl,ljg->djg",
        exponent_scores.astype(jnp.bfloat16),
        value_slice,
        preferred_element_type=jnp.float32,
    )
    attention_output = attention_output / jnp.transpose(softmax_total)[:, :, None]
    blended_rows = jnp.concatenate(
        [attention_output.astype(jnp.bfloat16), prepared[..., 3 * head_dim :]], axis=-1
    )
    combined_output = lax.all_gather(out_local, "frames", axis=1, tiled=True)
    summed = lax.psum_scatter(
        jnp.einsum(
            "vto,ox->vtx", blended_rows, combined_output, preferred_element_type=jnp.float32
        ).astype(jnp.bfloat16),
        "tensor",
        scatter_dimension=0,
        tiled=True,
    ).astype(jnp.float32)
    return (patches.astype(jnp.float32) + summed).astype(jnp.bfloat16)


def solution(mesh):
    return jax.shard_map(
        local,
        mesh=mesh,
        in_specs=(
            P("tensor", ("groups", "frames"), None),
            P(),
            P("frames", "tensor", None),
            P("tensor", None),
            P("tensor", None),
            P("tensor", None, "frames"),
        ),
        out_specs=P("tensor", ("groups", "frames"), None),
        check_vma=False,
    )
```

profile of v0, /device:TPU:0, one launch (start us, length us, event | category | flops | bytes accessed | tf_op | source)
XLA Modules:
  0.0 220.3 jit_solution(9089769881547310153)
XLA Ops:
  6.5 0.0 copy-start
  6.5 0.0 copy-start.1
  6.5 0.0 all-gather.6.cloned.1.call-start
  6.5 1.4 convert_reduce_fusion
  7.9 1.5 fusion.5
  9.5 0.0 copy-done
  9.5 0.0 copy-done.1
  9.5 1.2 fusion.7
  10.7 0.0 all-gather.6.cloned.1.call-update
  10.7 0.0 all-gather.8.cloned.1.call-start
  10.8 0.7 all-gather.8.cloned.1.call-update
  11.5 0.0 all-gather.10.cloned.1.call-start
  11.5 0.7 all-gather.10.cloned.1.call-update
  12.2 0.0 copy-start.2
  12.2 0.0 copy-start.3
  12.2 0.0 reduce-scatter.2.cloned.1.call-start
  12.3 64.8 %all-gather.6.cloned.1.call-done = bf16[256,2,3072]{2,0,1:T(8,128)(2,1)} async-done(((bf16[64,2,3072]{2,0,1:T(8,128)(2,1)}), bf16[256,2,3072]{2,0,1:T(8,128)(2,1)}) %all-gather.6.cloned.1.call-update) | async-done | bytes 3145744 | tf_op jit(solution)/shard_map/all_gather | solution.py:20
  77.0 37.7 %all-gather.8.cloned.1.call-done = bf16[3072,1,768]{2,0,1:T(8,128)(2,1)} async-done(((bf16[768,1,768]{2,0,1:T(8,128)(2,1)}), bf16[3072,1,768]{2,0,1:T(8,128)(2,1)}) %all-gather.8.cloned.1.call-update) | async-done | bytes 4718608 | tf_op jit(solution)/shard_map/all_gather | solution.py:24
  114.7 5.9 %fusion = f32[256,2,768]{2,0,1:T(8,128)S(1)} fusion(bf16[256,2,3072]{2,0,1:T(8,128)(2,1)} %all-gather.6.cloned.1.call-done, bf16[3072,1,768]{2,0,1:T(8,128)(2,1)} %all-gather.8.cloned.1.call-done), kind=kOutput, calls=%fused_computation | convolution fusion | flops 2415919104 | bytes 9437184 | tf_op jit(solution)/shard_map/qye,ea->qya/dot_general | solution.py:21
  120.6 0.2 slice_reduce_fusion.1
  120.8 0.4 multiply_reduce_fusion.1
  121.2 0.0 copy-done.2
  121.3 0.0 copy-done.3
  121.3 0.5 fusion.33
  121.8 0.3 fusion.11
  122.0 1.7 fusion.14
  123.8 21.1 %all-gather.10.cloned.1.call-done = bf16[1,512,3072]{2,1,0:T(8,128)(2,1)} async-done(((bf16[1,512,768]{2,1,0:T(8,128)(2,1)}), bf16[1,512,3072]{2,1,0:T(8,128)(2,1)}) %all-gather.10.cloned.1.call-update) | async-done | bytes 3145744 | tf_op jit(solution)/shard_map/all_gather | solution.py:52
  144.8 5.4 %convolution_convert_fusion = bf16[256,2,3072]{2,0,1:T(8,128)(2,1)} fusion(bf16[1,512,3072]{2,1,0:T(8,128)(2,1)} %all-gather.10.cloned.1.call-done, bf16[256,2,384]{2,0,1:T(8,128)(2,1)S(1)} %fusion.14, bf16[256,2,128]{2,0,1:T(8,128)(2,1)S(1)} %fusion.11), kind=kOutput, calls=%fused_computation.2 | convolution fusion | flops 1613234176 | bytes 6815744 | tf_op jit(solution)/shard_map/vto,ox->vtx/dot_general | solution.py:54
  150.2 0.0 reduce-scatter.2.cloned.1.call-update
  150.2 60.6 %reduce-scatter.2.cloned.1.call-done = bf16[64,2,3072]{2,0,1:T(8,128)(2,1)} async-done(((bf16[256,2,3072]{2,0,1:T(8,128)(2,1)}), bf16[64,2,3072]{2,0,1:T(8,128)(2,1)}) %reduce-scatter.2.cloned.1.call-update) | async-done | bytes 786448 | tf_op jit(solution)/shard_map/reduce_scatter | solution.py:53
  210.8 1.3 fusion.8
  212.1 1.7 copy.8
  (5 shorter events, 0.0 us)
Async XLA Ops:
  6.5 2.9 %copy-start = (bf16[64,2,3072]{2,1,0:T(2,128)(2,1)S(1)}, bf16[64,2,3072]{2,1,0:T(2,128)(2,1)}, u32[]{:S(2)}) copy-start(bf16[64,2,3072]{2,1,0:T(2,128)(2,1)} %param.6) | copy-start | bytes 2359300
  6.5 2.9 %copy-start.1 = (f32[3072]{0:T(1024)S(1)}, f32[3072]{0:T(1024)}, u32[]{:S(2)}) copy-start(f32[3072]{0:T(1024)} %param.7) | copy-start | bytes 36868
  6.5 70.5 %all-gather.6.cloned.1.call-start = ((), (), s32[]{:S(2)}) async-start(), calls=%async_computation.1 | async-start | bytes 3932160 | tf_op jit(solution)/shard_map/all_gather | solution.py:20
  10.7 104.0 %all-gather.8.cloned.1.call-start = ((), (), s32[]{:S(2)}) async-start(), calls=%async_computation.3 | async-start | bytes 5898240 | tf_op jit(solution)/shard_map/all_gather | solution.py:24
  11.5 133.3 %all-gather.10.cloned.1.call-start = ((), (), s32[]{:S(2)}) async-start(), calls=%async_computation.4 | async-start | bytes 3932160 | tf_op jit(solution)/shard_map/all_gather | solution.py:52
  12.2 109.0 %copy-start.2 = (f32[1,128]{1,0:T(1,128)S(1)}, f32[1,128]{1,0:T(1,128)}, u32[]{:S(2)}) copy-start(f32[1,128]{1,0:T(1,128)} %param.10) | copy-start | bytes 1540
  12.2 109.0 %copy-start.3 = (f32[1,128]{1,0:T(1,128)S(1)}, f32[1,128]{1,0:T(1,128)}, u32[]{:S(2)}) copy-start(f32[1,128]{1,0:T(1,128)} %param.9) | copy-start | bytes 1540
  12.2 198.5 %reduce-scatter.2.cloned.1.call-start = ((), (), s32[]{:S(2)}) async-start(), calls=%async_computation.2 | async-start | bytes 3932160 | tf_op jit(solution)/shard_map/reduce_scatter | solution.py:53
Sparse Core Ops, SparseCore 0:
  10.8 66.1 all-gather.5
  78.6 36.0 all-gather.7
  116.3 28.5 all-gather.9
  150.3 60.3 reduce-scatter.1
where the time goes:
time: 221 us; the launch traced here: 220 us
  waiting for transfers between devices  185 us (84%)
  between operations  13.2 us (6%)
  matrix products  12 us (5%)
  other arithmetic  7.81 us (4%)
    all_gather x1, waiting for transfers between devices, local(): every_patch = lax.all_gather(normed, 'tensor', axis=0, tiled=True)  64.8 us
    reduce_scatter x1, waiting for transfers between devices, local(): lax.psum_scatter(jnp.einsum('vto,ox->vtx', blended_rows, combined_output,...  60.6 us
    all_gather x1, waiting for transfers between devices, local(): lax.all_gather(in_local, 'frames', axis=0, tiled=True)  37.7 us
    all_gather x1, waiting for transfers between devices, local(): combined_output = lax.all_gather(out_local, 'frames', axis=1, tiled=True)  21.1 us
    dot_general x1, matrix products, local(): jnp.einsum('qye,ea->qya', every_patch, lax.all_gather(in_local, 'frames',...  5.89 us
    dot_general x1, matrix products, local(): jnp.einsum('vto,ox->vtx', blended_rows, combined_output, preferred_elemen...  5.36 us
  transfers between devices with their start and end apart: 4, of which 4 were waited for; matrix products, arithmetic and copies ran while one was open for 4% of the time, Pallas kernels for 0%

commit v1 on v0

--- a/solution.py
+++ b/solution.py
@@ -49,7 +49,14 @@
     blended_rows = jnp.concatenate(
         [attention_output.astype(jnp.bfloat16), prepared[..., 3 * head_dim :]], axis=-1
     )
-    combined_output = lax.all_gather(out_local, "frames", axis=1, tiled=True)
+    size = lax.axis_size("frames")
+    hops = [(i, (i + 1) % size) for i in range(size)]
+    terms = [out_local]
+    for stride in range(1, size):
+        terms = [lax.ppermute(terms[0], "frames", hops), *terms]
+    whole = jnp.concatenate(terms, axis=1)
+    shift = (lax.axis_index("frames") + 1) * terms[-1].shape[1]
+    combined_output = jnp.roll(whole, shift, axis=1)
     summed = lax.psum_scatter(
         jnp.einsum(
             "vto,ox->vtx", blended_rows, combined_output, preferred_element_type=jnp.float32

time: 221 us -> 201 us (0.910)
  waiting for transfers between devices: 185 us -> 156 us
  local copies, waits for them, and re-layouts: 1.71 us -> 9.62 us
    all_gather x1, waiting for transfers between devices: 64.8 us -> 22.6 us  [local(): every_patch = lax.all_gather(normed, 'tensor', axis=0, tiled=True)]
    ppermute x0 -> x3, waiting for transfers between devices: none -> 34.4 us  [local(): terms = [lax.ppermute(terms[0], 'frames', hops), *terms]]
    all_gather x1 -> x0, waiting for transfers between devices: 21.1 us -> none  [local(): combined_output = lax.all_gather(out_local, 'frames', axis=1, tiled=True)]
    unnamed x8 -> x15, local copies, waits for them, and re-layouts: 0.02 us -> 6.94 us
  transfers between devices with their start and end apart: 4 -> 6, of which waited for: 4 -> 6; matrix products, arithmetic and copies ran while one was open for 4% -> 4% of each run, Pallas kernels for 0% -> 0%
where the time goes in v1:
time: 201 us
  waiting for transfers between devices  156 us (78%)
  between operations  13.2 us (7%)
  matrix products  12.2 us (6%)
  local copies, waits for them, and re-layouts  9.62 us (5%)
  other arithmetic  8.96 us (4%)
    reduce_scatter x1, waiting for transfers between devices, local(): lax.psum_scatter(jnp.einsum('vto,ox->vtx', blended_rows, combined_output,...  60.6 us
    all_gather x1, waiting for transfers between devices, local(): lax.all_gather(in_local, 'frames', axis=0, tiled=True)  37.7 us
    ppermute x3, waiting for transfers between devices, local(): terms = [lax.ppermute(terms[0], 'frames', hops), *terms]  34.4 us
    all_gather x1, waiting for transfers between devices, local(): every_patch = lax.all_gather(normed, 'tensor', axis=0, tiled=True)  22.6 us
    unnamed x15, local copies, waits for them, and re-layouts  6.94 us
    dot_general x1, matrix products, local(): jnp.einsum('qye,ea->qya', every_patch, lax.all_gather(in_local, 'frames',...  5.89 us
    dot_general x1, matrix products, local(): jnp.einsum('vto,ox->vtx', blended_rows, combined_output, preferred_elemen...  5.55 us
  transfers between devices with their start and end apart: 6, of which 6 were waited for; matrix products, arithmetic and copies ran while one was open for 4% of the time, Pallas kernels for 0%

profile of v1, /device:TPU:0, one launch (start us, length us, event | category | flops | bytes accessed | tf_op | source)
XLA Modules:
  0.0 200.6 jit_solution(6290788865916196688)
XLA Ops:
  6.5 1.4 convert_reduce_fusion
  7.9 1.5 fusion.6
  9.5 2.4 %fusion.8 = bf16[64,2,3072]{2,0,1:T(8,128)(2,1)} fusion(f32[3072]{0:T(1024)} %param.7, f32[64,2]{0,1:T(2,128)S(1)} %add_rsqrt_fusion.2, f32[64,2]{0,1:T(2,128)S(1)} %broadcast_multiply_fusion.2, bf16[64,2,3072]{2,1,0:T(2,128)(2,1)} %param.6), kind=kLoop, calls=%fused_computation.12 | loop fusion | flops 1966080 | bytes 1586176 | tf_op jit(solution)/shard_map/convert_element_type | solution.py:17
  11.8 0.0 all-gather.4.cloned.1.call-update
  11.9 0.0 all-gather.6.cloned.1.call-start
  11.9 0.7 all-gather.6.cloned.1.call-update
  12.6 0.0 reduce-scatter.2.cloned.1.call-start
  12.7 0.5 collective-permute-start
  13.2 11.6 %collective-permute-done = bf16[512,768]{1,0:T(8,128)(2,1)S(1)} collective-permute-done((bf16[512,768]{1,0:T(8,128)(2,1)S(1)}, bf16[512,768]{1,0:T(8,128)(2,1)S(1)}, u32[]{:S(2)}, u32[]{:S(2)}) %collective-permute-start) | collective-permute-done | bytes 786464 | tf_op jit(solution)/shard_map/ppermute | solution.py:56
  24.8 11.4 %collective-permute-done.1 = bf16[512,768]{1,0:T(8,128)(2,1)S(1)} collective-permute-done((bf16[512,768]{1,0:T(8,128)(2,1)S(1)}, bf16[512,768]{1,0:T(8,128)(2,1)S(1)}, u32[]{:S(2)}, u32[]{:S(2)}) %collective-permute-start.1) | collective-permute-done | bytes 786464 | tf_op jit(solution)/shard_map/ppermute | solution.py:56
  36.2 11.4 %collective-permute-done.2 = bf16[512,768]{1,0:T(8,128)(2,1)S(1)} collective-permute-done((bf16[512,768]{1,0:T(8,128)(2,1)S(1)}, bf16[512,768]{1,0:T(8,128)(2,1)S(1)}, u32[]{:S(2)}, u32[]{:S(2)}) %collective-permute-start.2) | collective-permute-done | bytes 786464 | tf_op jit(solution)/shard_map/ppermute | solution.py:56
  47.6 1.0 constant_dynamic-update-slice_fusion.7
  48.6 1.0 constant_dynamic-update-slice_fusion.6
  49.6 1.0 constant_dynamic-update-slice_fusion.5
  50.6 1.0 constant_dynamic-update-slice_fusion.4
  51.6 1.0 constant_dynamic-update-slice_fusion.3
  52.6 1.0 constant_dynamic-update-slice_fusion.2
  53.6 1.0 constant_dynamic-update-slice_fusion.1
  54.6 1.0 constant_dynamic-update-slice_fusion
  55.6 22.6 %all-gather.4.cloned.1.call-done = bf16[256,2,3072]{2,0,1:T(8,128)(2,1)} async-done(((bf16[64,2,3072]{2,0,1:T(8,128)(2,1)}), bf16[256,2,3072]{2,0,1:T(8,128)(2,1)}) %all-gather.4.cloned.1.call-update) | async-done | bytes 3145744 | tf_op jit(solution)/shard_map/all_gather | solution.py:20
  78.2 37.7 %all-gather.6.cloned.1.call-done = bf16[3072,1,768]{2,0,1:T(8,128)(2,1)} async-done(((bf16[768,1,768]{2,0,1:T(8,128)(2,1)}), bf16[3072,1,768]{2,0,1:T(8,128)(2,1)}) %all-gather.6.cloned.1.call-update) | async-done | bytes 4718608 | tf_op jit(solution)/shard_map/all_gather | solution.py:24
  115.9 5.9 %fusion = f32[256,2,768]{2,0,1:T(8,128)S(1)} fusion(bf16[256,2,3072]{2,0,1:T(8,128)(2,1)} %all-gather.4.cloned.1.call-done, bf16[3072,1,768]{2,0,1:T(8,128)(2,1)} %all-gather.6.cloned.1.call-done), kind=kOutput, calls=%fused_computation | convolution fusion | flops 2415919104 | bytes 9437184 | tf_op jit(solution)/shard_map/qye,ea->qya/dot_general | solution.py:21
  121.7 0.2 slice_reduce_fusion.1
  122.0 1.7 fusion.15
  123.7 0.4 multiply_reduce_fusion.1
  124.1 0.5 fusion.35
  124.6 0.3 fusion.12
  124.9 5.6 %convolution_convert_fusion = bf16[256,2,3072]{2,0,1:T(8,128)(2,1)} fusion(bf16[512,6144]{1,0:T(8,128)(2,1)} %constant_dynamic-update-slice_fusion, s32[]{:T(128)S(6)} %select_n.14, bf16[256,2,384]{2,0,1:T(8,128)(2,1)S(1)} %fusion.15, bf16[256,2,128]{2,0,1:T(8,128)(2,1)S(1)} %fusion.12), kind=kOutput, calls=%fused_computation.2 | convolution fusion | flops 1613234176 | bytes 6815748 | tf_op jit(solution)/shard_map/vto,ox->vtx/dot_general | solution.py:61
  130.5 0.0 reduce-scatter.2.cloned.1.call-update
  130.5 60.6 %reduce-scatter.2.cloned.1.call-done = bf16[64,2,3072]{2,0,1:T(8,128)(2,1)} async-done(((bf16[256,2,3072]{2,0,1:T(8,128)(2,1)}), bf16[64,2,3072]{2,0,1:T(8,128)(2,1)}) %reduce-scatter.2.cloned.1.call-update) | async-done | bytes 786448 | tf_op jit(solution)/shard_map/reduce_scatter | solution.py:60
  191.0 1.3 fusion.9
  192.4 1.7 copy.8
  (16 shorter events, 0.1 us)
Async XLA Ops:
  6.5 6.1 %copy-start.1 = (bf16[1,512,768]{2,1,0:T(8,128)(2,1)S(1)}, bf16[1,512,768]{2,1,0:T(8,128)(2,1)}, u32[]{:S(2)}) copy-start(bf16[1,512,768]{2,1,0:T(8,128)(2,1)} %param.11) | copy-start | bytes 2359300
  6.5 71.7 %all-gather.4.cloned.1.call-start = ((), (), s32[]{:S(2)}) async-start(), calls=%async_computation.1 | async-start | bytes 3932160 | tf_op jit(solution)/shard_map/all_gather | solution.py:20
  11.9 104.0 %all-gather.6.cloned.1.call-start = ((), (), s32[]{:S(2)}) async-start(), calls=%async_computation.3 | async-start | bytes 5898240 | tf_op jit(solution)/shard_map/all_gather | solution.py:24
  12.6 178.4 %reduce-scatter.2.cloned.1.call-start = ((), (), s32[]{:S(2)}) async-start(), calls=%async_computation.2 | async-start | bytes 3932160 | tf_op jit(solution)/shard_map/reduce_scatter | solution.py:60
  12.7 12.1 %collective-permute-start = (bf16[512,768]{1,0:T(8,128)(2,1)S(1)}, bf16[512,768]{1,0:T(8,128)(2,1)S(1)}, u32[]{:S(2)}, u32[]{:S(2)}) collective-permute-start(bf16[512,768]{1,0:T(8,128)(2,1)S(1)} %bitcast.21), channel_id=1, source_target_pairs={{0,1},{1,2},{2,3},{3,0},{4,5},{5,6},{6,7},{7,4},{8,9},{9,10},{10,1... | collective-permute-start | bytes 2359304 | tf_op jit(solution)/shard_map/ppermute | solution.py:56
  24.8 11.4 %collective-permute-start.1 = (bf16[512,768]{1,0:T(8,128)(2,1)S(1)}, bf16[512,768]{1,0:T(8,128)(2,1)S(1)}, u32[]{:S(2)}, u32[]{:S(2)}) collective-permute-start(bf16[512,768]{1,0:T(8,128)(2,1)S(1)} %collective-permute-done), channel_id=1, source_target_pairs={{0,1},{1,2},{2,3},{3,0},{4,5},{5,6},{6,7},{7,4},{8,9},{9,10},{10,1... | collective-permute-start | bytes 2359304 | tf_op jit(solution)/shard_map/ppermute | solution.py:56
  36.2 11.4 %collective-permute-start.2 = (bf16[512,768]{1,0:T(8,128)(2,1)S(1)}, bf16[512,768]{1,0:T(8,128)(2,1)S(1)}, u32[]{:S(2)}, u32[]{:S(2)}) collective-permute-start(bf16[512,768]{1,0:T(8,128)(2,1)S(1)} %collective-permute-done.1), channel_id=1, source_target_pairs={{0,1},{1,2},{2,3},{3,0},{4,5},{5,6},{6,7},{7,4},{8,9},{9,10},{10,1... | collective-permute-start | bytes 2359304 | tf_op jit(solution)/shard_map/ppermute | solution.py:56
  55.6 68.5 %copy-start.2 = (f32[1,128]{1,0:T(1,128)S(1)}, f32[1,128]{1,0:T(1,128)}, u32[]{:S(2)}) copy-start(f32[1,128]{1,0:T(1,128)} %param.10) | copy-start | bytes 1540
  55.6 68.5 %copy-start.3 = (f32[1,128]{1,0:T(1,128)S(1)}, f32[1,128]{1,0:T(1,128)}, u32[]{:S(2)}) copy-start(f32[1,128]{1,0:T(1,128)} %param.9) | copy-start | bytes 1540
  130.5 60.6 %copy-start = (bf16[64,2,3072]{2,1,0:T(2,128)(2,1)S(1)}, bf16[64,2,3072]{2,1,0:T(2,128)(2,1)}, u32[]{:S(2)}) copy-start(bf16[64,2,3072]{2,1,0:T(2,128)(2,1)} %param.6) | copy-start | bytes 2359300
Sparse Core Ops, SparseCore 0:
  12.0 66.1 all-gather.3
  79.7 36.0 all-gather.5
  130.6 60.3 reduce-scatter.1
